TPU v7x, 32 devices: a whole 2x2x4 slice. The times are simulated.
32 devices in a mesh: grp: 2 (over x), lat: 16 (over z, y, core).
Axes of the slice: x: 2, y: 2, z: 4, core: 2. Of those that a mesh axis runs over, the one named last changes fastest.
Arguments:
- acts: bfloat16 [128, 2, 2048], P(('grp', 'lat')), parts along dimension 0, may hold values from -6 to 6
- enc_weight: bfloat16 [4, 2048, 4096], P('grp', None, 'lat'), parts along dimension 0, may hold values from -0.09375 to 0.09375
- enc_bias: float32 [8192], P(('grp', 'lat')), parts along dimension 0, may hold values from -3 to 3
- dec_weight: bfloat16 [4096, 4, 2048], P('lat', 'grp'), parts along dimension 1, may hold values from -0.125 to 0.125
- dec_bias: float32 [4, 2048], P('grp'), parts along dimension 0, may hold values from -5 to 5
Outputs:
- residual: bfloat16 [128, 2, 2048], P(('grp', 'lat')), parts along dimension 0
- grad_enc: bfloat16 [4, 2048, 4096], P('grp', None, 'lat'), parts along dimension 0
- grad_enc_bias: float32 [8192], P(('grp', 'lat')), parts along dimension 0
- grad_dec: bfloat16 [4096, 4, 2048], P('lat', 'grp'), parts along dimension 1
- grad_dec_bias: float32 [4, 2048], P('grp'), parts along dimension 0
There are 2 independent parts, one for each index of `grp`. A program takes and returns all parts, laid end to end along the dimension named above; each array names one. Nothing has to cross between parts.
All inputs are finite; a program needn't handle non-finite values.
Results may differ from a plain program's by a relative error of at most 0.015.
Values may be sent and summed in bfloat16 or wider, within the bound.
No kernel may reach another device: no remote copies, remote signals or barrier semaphores. Data moves between devices by JAX's collectives and lax.ppermute only.
A program may use at most 128 MiB of HBM per device.

v0:
```python
import jax
import jax.numpy as jnp
from jax import lax
from jax.sharding import PartitionSpec as P

sparsity_weight = 2.0


def body(acts, enc_weight, enc_bias, dec_weight, dec_bias):
    tok_dev, layers, width = acts.shape
    lat_dev = enc_weight.shape[2]
    wide = layers * width
    total_rows = tok_dev * lax.axis_size("lat")
    factor = 2.0 / total_rows
    flat_rows = acts.reshape(tok_dev, wide)
    flat_enc = enc_weight.reshape(wide, lat_dev)
    flat_dec = dec_weight.reshape(lat_dev, wide)
    flat_bias = dec_bias.reshape(wide)
    own_start = lax.axis_index("lat") * tok_dev
    gathered = lax.all_gather(flat_rows, "lat", axis=0, tiled=True)
    before = jnp.dot(gathered, flat_enc, preferred_element_type=jnp.float32) + enc_bias
    active = jnp.maximum(before, 0.0).astype(jnp.bfloat16)
    dec_wide = dec_weight.astype(jnp.float32)
    row_sq = jnp.sum(dec_wide * dec_wide, axis=2)
    inv_norm = lax.rsqrt(row_sq + 1.0)
    dec_norm = jnp.sum(jnp.sqrt(row_sq + 1.0), axis=1)
    term = jnp.dot(active, flat_dec, preferred_element_type=jnp.float32)
    own_term = lax.dynamic_slice_in_dim(term, own_start, tok_dev, 0)
    own_term = own_term + flat_bias - flat_rows.astype(jnp.float32)
    term = lax.dynamic_update_slice_in_dim(term, own_term, own_start, 0)
    summed = lax.psum(term, "lat")
    all_residual = summed.astype(jnp.bfloat16)
    own_residual = lax.dynamic_slice_in_dim(all_residual, own_start, tok_dev, 0)
    grad_dec_bias = factor * jnp.sum(all_residual.astype(jnp.float32), axis=0)
    dec_total = lax.dot_general(
        active, all_residual, (((0,), (0,)), ((), ())), preferred_element_type=jnp.float32
    )
    backward = lax.dot_general(
        all_residual, flat_dec, (((1,), (1,)), ((), ())), preferred_element_type=jnp.float32
    )
    grad_act = factor * backward + sparsity_weight / total_rows * dec_norm
    grad_before = jnp.where(before > 0.0, grad_act, 0.0).astype(jnp.bfloat16)
    enc_total = lax.dot_general(
        gathered, grad_before, (((0,), (0,)), ((), ())), preferred_element_type=jnp.float32
    )
    grad_enc = enc_total.astype(jnp.bfloat16).reshape(layers, width, lat_dev)
    grad_enc_bias = jnp.sum(grad_before.astype(jnp.float32), axis=0)
    act_sum = jnp.sum(active.astype(jnp.float32), axis=0)
    grad_dec = (
        factor * dec_total.reshape(lat_dev, layers, width)
        + sparsity_weight / total_rows * act_sum[:, None, None] * dec_wide * inv_norm[:, :, None]
    ).astype(jnp.bfloat16)
    return (
        own_residual.reshape(tok_dev, layers, width),
        grad_enc,
        grad_enc_bias,
        grad_dec,
        grad_dec_bias.reshape(layers, width),
    )


def solution(mesh):
    return jax.shard_map(
        body,
        mesh=mesh,
        in_specs=(
            P(("grp", "lat"), None, None),
            P("grp", None, "lat"),
            P(("grp", "lat")),
            P("lat", "grp", None),
            P("grp", None),
        ),
        out_specs=(
            P(("grp", "lat"), None, None),
            P("grp", None, "lat"),
            P(("grp", "lat")),
            P("lat", "grp", None),
            P("grp", None),
        ),
        check_vma=False,
    )
```

profile of v0, /device:TPU:0, one launch (start us, length us, event | category | flops | bytes accessed | tf_op | source)
XLA Modules:
  0.0 136.5 jit_solution(2590079693091624209)
XLA Ops:
  0.6 0.0 copy-start
  0.7 1.6 %copy-done = bf16[2,2048,256]{2,1,0:T(8,128)(2,1)S(1)} copy-done((bf16[2,2048,256]{2,1,0:T(8,128)(2,1)S(1)}, bf16[2,2048,256]{2,1,0:T(8,128)(2,1)}, u32[]{:S(2)}) %copy-start) | copy-done | bytes 2097176
  2.2 0.7 copy.14
  2.9 0.8 reshape.50
  3.7 0.8 convert_bitcast_fusion
  4.5 0.0 copy-start.3
  4.6 3.8 %fusion.1 = f32[256,2]{1,0:T(8,128)S(1)} fusion(bf16[256,2,2048]{2,1,0:T(2,128)(2,1)} %param.8), kind=kLoop, calls=%fused_computation.5 | loop fusion | flops 3145216 | bytes 2099200 | tf_op jit(solution)/shard_map/reduce_sum | solution.py:24
  8.4 0.1 add_rsqrt_fusion
  8.6 24.6 %all-gather = bf16[16,4,4096]{2,1,0:T(4,128)(2,1)S(1)} all-gather(bf16[1,4,4096]{2,1,0:T(4,128)(2,1)S(1)} %reshape.50), channel_id=1, replica_groups=mesh['grp'=2,'lat'=16] {'lat'}, dimensions={0}, use_global_device_ids=true | all-gather | bytes 557056 | tf_op jit(solution)/shard_map/all_gather | solution.py:20
  33.2 0.1 reshape.51
  33.3 0.0 copy-done.3
  33.3 0.0 copy-start.1
  33.3 0.5 convert_reduce_fusion.1
  33.8 1.1 copy-done.1
  34.9 0.9 copy.13
  35.8 0.0 copy-start.2
  35.8 1.3 copy-done.2
  37.1 1.5 %fusion.8 = f32[64,4096]{1,0:T(8,128)} fusion(bf16[256,4096]{1,0:T(8,128)(2,1)S(1)} %bitcast.21, f32[64,256]{1,0:T(8,128)S(1)} %get-tuple-element.20), kind=kOutput, calls=%fused_computation.26 | convolution fusion | flops 134250496 | bytes 3211264 | tf_op jit(solution)/shard_map/dot_general | solution.py:27
  38.6 1.6 %subtract_dynamic-update-slice_fusion = f32[64,4096]{1,0:T(8,128)} fusion(f32[64,4096]{1,0:T(8,128)} %fusion.8, s32[]{:T(128)S(6)} %select_n.9, f32[4,4096]{1,0:T(4,128)S(1)} %bitcast.24, f32[4096]{0:T(1024)S(1)} %bitcast.25), kind=kLoop, calls=%fused_computation.20 | loop fusion | flops 32768 | bytes 212996 | tf_op jit(solution)/shard_map/dynamic_update_slice | solution.py:30
  40.1 70.1 %all-reduce.1 = bf16[64,4096]{1,0:T(8,128)(2,1)S(1)} all-reduce(f32[64,4096]{1,0:T(8,128)} %subtract_dynamic-update-slice_fusion), channel_id=1, replica_groups=mesh['grp'=2,'lat'=16] {'lat'}, use_global_device_ids=true, to_apply=%region_0.0 | all-reduce | flops 262144 | bytes 1572864 | tf_op jit(solution)/shard_map/psum | solution.py:31
  110.2 2.9 %convert_reduce_fusion.2 = (f32[256]{0:T(256)}, bf16[64,256]{1,0:T(8,128)(2,1)S(1)}) fusion(f32[256]{0:T(256)S(1)} %broadcast_multiply_fusion.2, bf16[64,4096]{1,0:T(8,128)(2,1)S(1)} %all-reduce.1, bf16[256,4096]{1,0:T(8,128)(2,1)} %bitcast.22, f32[64,256]{1,0:T(8,128)S(1)} %get-tuple-element.20), kind=kOutput, calls=%fused_computation.19 | convolution fusion | flops 134332160 | bytes 2721792 | tf_op jit(solution)/shard_map/dot_general | solution.py:38
  113.1 0.1 convert_reduce_fusion
  113.3 0.6 mul.82
  113.9 0.7 reshape.48
  114.6 2.0 %fusion = bf16[4096,256]{0,1:T(8,128)(2,1)} fusion(bf16[64,256]{1,0:T(8,128)(2,1)S(1)} %get-tuple-element.18, bf16[64,4096]{1,0:T(8,128)(2,1)S(1)} %reshape.51), kind=kOutput, calls=%fused_computation.4 | convolution fusion | flops 135266304 | bytes 2654208 | tf_op jit(solution)/shard_map/dot_general | solution.py:43
  116.6 4.1 %copy.12 = bf16[4096,256]{1,0:T(8,128)(2,1)} copy(bf16[4096,256]{0,1:T(8,128)(2,1)} %fusion) | data formatting | bytes 4194304
  120.7 2.7 %convolution_multiply_fusion = f32[256,4096]{1,0:T(8,128)} fusion(bf16[64,4096]{1,0:T(8,128)(2,1)S(1)} %all-reduce.1, f32[64,256]{1,0:T(8,128)S(1)} %get-tuple-element.20), kind=kOutput, calls=%fused_computation | convolution fusion | flops 135299072 | bytes 4784128 | tf_op jit(solution)/shard_map/dot_general | solution.py:35
  123.3 6.6 %mul.74 = f32[256,2,2048]{2,1,0:T(2,128)} reshape(f32[256,4096]{1,0:T(8,128)} %convolution_multiply_fusion) | data formatting | bytes 8388608 | tf_op jit(solution)/shard_map/mul | solution.py:50
  129.9 6.7 %fusion.4 = bf16[256,2,2048]{2,1,0:T(2,128)(2,1)} fusion(f32[256,2,2048]{2,1,0:T(2,128)} %mul.74, bf16[256,2,2048]{2,1,0:T(2,128)(2,1)} %param.8, f32[256]{0:T(256)S(1)} %broadcast_multiply_fusion.1, f32[256,2]{1,0:T(8,128)S(1)} %get-tuple-element.15), kind=kLoop, calls=%fused_computation.8 | loop fusion | flops 5242880 | bytes 8391680 | tf_op jit(solution)/shard_map/convert_element_type | solution.py:52
  (5 shorter events, 0.1 us)
Async XLA Ops:
  0.6 1.6 %copy-start = (bf16[2,2048,256]{2,1,0:T(8,128)(2,1)S(1)}, bf16[2,2048,256]{2,1,0:T(8,128)(2,1)}, u32[]{:S(2)}) copy-start(bf16[2,2048,256]{2,1,0:T(8,128)(2,1)} %param.6) | copy-start | bytes 6291460
  4.5 28.8 %copy-start.3 = (f32[256]{0:T(256)S(1)}, f32[256]{0:T(256)}, u32[]{:S(2)}) copy-start(f32[256]{0:T(256)} %param.7) | copy-start | bytes 3076
  33.3 1.6 %copy-start.1 = (bf16[256,2,2048]{2,1,0:T(2,128)(2,1)S(1)}, bf16[256,2,2048]{2,1,0:T(2,128)(2,1)}, u32[]{:S(2)}) copy-start(bf16[256,2,2048]{2,1,0:T(2,128)(2,1)} %param.8) | copy-start | bytes 6291460
  35.8 1.3 copy-start.2
where the time goes:
time: 137 us
  blocking collectives  94.7 us (69%)
  local copies, waits for them, and re-layouts  18.5 us (14%)
  other arithmetic  13.1 us (10%)
  matrix products  9.56 us (7%)
    psum x1, blocking collectives, body(): summed = lax.psum(term, 'lat')  70.1 us
    all_gather x1, blocking collectives, body(): gathered = lax.all_gather(flat_rows, 'lat', axis=0, tiled=True)  24.6 us
    unnamed x14, local copies, waits for them, and re-layouts  10.6 us
    convert_element_type x1, other arithmetic, body(): grad_dec = (factor * dec_total.reshape(lat_dev, layers, width) + sparsity...  6.65 us
    mul x1, local copies, waits for them, and re-layouts, body(): factor * dec_total.reshape(lat_dev, layers, width)  6.57 us
    reduce_sum x1, other arithmetic, body(): row_sq = jnp.sum(dec_wide * dec_wide, axis=2)  3.84 us
    dot_general x1, matrix products, body(): lax.dot_general(all_residual, flat_dec, (((1,), (1,)), ((), ())), preferr...  2.94 us

commit v1 on v0

--- a/solution.py
+++ b/solution.py
@@ -28,7 +28,13 @@
     own_term = lax.dynamic_slice_in_dim(term, own_start, tok_dev, 0)
     own_term = own_term + flat_bias - flat_rows.astype(jnp.float32)
     term = lax.dynamic_update_slice_in_dim(term, own_term, own_start, 0)
-    summed = lax.psum(term, "lat")
+    summed = term
+    axis_total = lax.axis_size("lat")
+    for i in [
+        [(j, j ^ idx) for j in range(axis_total)] for idx in (1, 2, 4, 8, 16) if idx < axis_total
+    ]:
+        left_arr = lax.ppermute(summed, "lat", i)
+        summed = summed + left_arr
     all_residual = summed.astype(jnp.bfloat16)
     own_residual = lax.dynamic_slice_in_dim(all_residual, own_start, tok_dev, 0)
     grad_dec_bias = factor * jnp.sum(all_residual.astype(jnp.float32), axis=0)

time: 137 us -> 159 us (1.16)
  waiting for transfers between devices: 0 us -> 96.9 us
  blocking collectives: 94.7 us -> 24.6 us
  other arithmetic: 13.1 us -> 10.4 us
  matrix products: 9.56 us -> 6.99 us
    ppermute x0 -> x4, waiting for transfers between devices: none -> 96.9 us  [body(): left_arr = lax.ppermute(summed, 'lat', i)]
    psum x1 -> x0, blocking collectives: 70.1 us -> none  [body(): summed = lax.psum(term, 'lat')]
    reduce_sum x1, other arithmetic: 3.84 us -> 2.24 us  [body(): row_sq = jnp.sum(dec_wide * dec_wide, axis=2)]
    dot_general x1, matrix products: 2.94 us -> 1.34 us  [body(): lax.dot_general(all_residual, flat_dec, (((1,), (1,)), ((), ())), preferr...]
  transfers between devices with their start and end apart: 0 -> 4, of which waited for: 0 -> 4; matrix products, arithmetic and copies ran while one was open for 0% -> 1% of each run, Pallas kernels for 0% -> 0%
where the time goes in v1:
time: 159 us
  waiting for transfers between devices  96.9 us (61%)
  blocking collectives  24.6 us (15%)
  local copies, waits for them, and re-layouts  18.7 us (12%)
  other arithmetic  10.4 us (7%)
  matrix products  6.99 us (4%)
    ppermute x4, waiting for transfers between devices, body(): left_arr = lax.ppermute(summed, 'lat', i)  96.9 us
    all_gather x1, blocking collectives, body(): gathered = lax.all_gather(flat_rows, 'lat', axis=0, tiled=True)  24.6 us
    unnamed x14, local copies, waits for them, and re-layouts  10.8 us
    convert_element_type x1, other arithmetic, body(): grad_dec = (factor * dec_total.reshape(lat_dev, layers, width) + sparsity...  6.65 us
    mul x1, local copies, waits for them, and re-layouts, body(): factor * dec_total.reshape(lat_dev, layers, width)  6.57 us
  transfers between devices with their start and end apart: 4, of which 4 were waited for; matrix products, arithmetic and copies ran while one was open for 1% of the time, Pallas kernels for 0%

profile of v1, /device:TPU:0, one launch (start us, length us, event | category | flops | bytes accessed | tf_op | source)
XLA Modules:
  0.0 159.0 jit_solution(3781297722359845455)
XLA Ops:
  0.6 0.0 copy-start
  0.6 0.9 reshape.50
  1.6 0.8 convert_bitcast_fusion
  2.4 0.7 copy.14
  3.1 24.6 %all-gather = bf16[16,4,4096]{2,1,0:T(4,128)(2,1)S(1)} all-gather(bf16[1,4,4096]{2,1,0:T(4,128)(2,1)S(1)} %reshape.50), channel_id=1, replica_groups=mesh['grp'=2,'lat'=16] {'lat'}, dimensions={0}, use_global_device_ids=true | all-gather | bytes 557056 | tf_op jit(solution)/shard_map/all_gather | solution.py:20
  27.8 0.1 reshape.51
  27.9 0.0 copy-start.3
  27.9 3.8 %copy.13 = bf16[32,8,2,2048]{3,1,2,0:T(8,128)(2,1)} copy(bf16[32,8,2,2048]{3,2,1,0:T(2,128)(2,1)} %bitcast.20) | data formatting | bytes 4194304
  31.7 0.0 copy-done
  31.7 0.0 copy-start.2
  31.7 0.0 copy-done.3
  31.7 0.5 convert_reduce_fusion.1
  32.2 1.1 copy-done.2
  33.3 0.5 fusion.8
  33.8 0.4 collective-permute-start
  34.2 2.3 %collective-permute-done = f32[64,4096]{1,0:T(8,128)S(1)} collective-permute-done((f32[64,4096]{1,0:T(8,128)S(1)}, f32[64,4096]{1,0:T(8,128)S(1)}, u32[]{:S(2)}, u32[]{:S(2)}) %collective-permute-start) | collective-permute-done | bytes 1048608 | tf_op jit(solution)/shard_map/ppermute | solution.py:36
  36.6 0.1 add.60
  36.7 0.1 collective-permute-start.1
  36.8 25.4 %collective-permute-done.1 = f32[64,4096]{1,0:T(8,128)S(1)} collective-permute-done((f32[64,4096]{1,0:T(8,128)S(1)}, f32[64,4096]{1,0:T(8,128)S(1)}, u32[]{:S(2)}, u32[]{:S(2)}) %collective-permute-start.1) | collective-permute-done | bytes 1048608 | tf_op jit(solution)/shard_map/ppermute | solution.py:36
  62.2 0.1 add.61
  62.3 0.0 copy-start.1
  62.3 0.1 collective-permute-start.2
  62.4 24.5 %collective-permute-done.2 = f32[64,4096]{1,0:T(8,128)S(1)} collective-permute-done((f32[64,4096]{1,0:T(8,128)S(1)}, f32[64,4096]{1,0:T(8,128)S(1)}, u32[]{:S(2)}, u32[]{:S(2)}) %collective-permute-start.2) | collective-permute-done | bytes 1048608 | tf_op jit(solution)/shard_map/ppermute | solution.py:36
  87.0 0.1 add.62
  87.1 0.1 collective-permute-start.3
  87.2 0.0 copy-done.1
  87.2 2.2 %fusion.1 = f32[256,2]{1,0:T(8,128)S(1)} fusion(bf16[256,2,2048]{2,1,0:T(2,128)(2,1)S(1)} %copy-done.1), kind=kLoop, calls=%fused_computation.5 | loop fusion | flops 3145216 | bytes 2099200 | tf_op jit(solution)/shard_map/reduce_sum | solution.py:24
  89.4 0.1 add_rsqrt_fusion
  89.6 44.7 %collective-permute-done.3 = f32[64,4096]{1,0:T(8,128)S(1)} collective-permute-done((f32[64,4096]{1,0:T(8,128)S(1)}, f32[64,4096]{1,0:T(8,128)S(1)}, u32[]{:S(2)}, u32[]{:S(2)}) %collective-permute-start.3) | collective-permute-done | bytes 1048608 | tf_op jit(solution)/shard_map/ppermute | solution.py:36
  134.2 0.1 convert_reduce_fusion
  134.4 2.7 %convolution_multiply_fusion = f32[256,4096]{1,0:T(8,128)} fusion(bf16[64,4096]{1,0:T(8,128)(2,1)S(1)} %get-tuple-element.16, f32[64,256]{1,0:T(8,128)S(1)} %get-tuple-element.22), kind=kOutput, calls=%fused_computation | convolution fusion | flops 135299072 | bytes 4784128 | tf_op jit(solution)/shard_map/dot_general | solution.py:41
  137.0 1.3 convert_reduce_fusion.2
  138.4 0.6 mul.82
  139.0 0.7 reshape.48
  139.7 2.0 %fusion = bf16[4096,256]{0,1:T(8,128)(2,1)} fusion(bf16[64,256]{1,0:T(8,128)(2,1)S(1)} %get-tuple-element.20, bf16[64,4096]{1,0:T(8,128)(2,1)S(1)} %reshape.51), kind=kOutput, calls=%fused_computation.4 | convolution fusion | flops 135266304 | bytes 2654208 | tf_op jit(solution)/shard_map/dot_general | solution.py:49
  141.7 4.1 %copy.12 = bf16[4096,256]{1,0:T(8,128)(2,1)} copy(bf16[4096,256]{0,1:T(8,128)(2,1)} %fusion) | data formatting | bytes 4194304
  145.8 6.6 %mul.74 = f32[256,2,2048]{2,1,0:T(2,128)} reshape(f32[256,4096]{1,0:T(8,128)} %convolution_multiply_fusion) | data formatting | bytes 8388608 | tf_op jit(solution)/shard_map/mul | solution.py:56
  152.3 6.7 %fusion.4 = bf16[256,2,2048]{2,1,0:T(2,128)(2,1)} fusion(f32[256,2,2048]{2,1,0:T(2,128)} %mul.74, bf16[256,2,2048]{2,1,0:T(2,128)(2,1)} %param.8, f32[256]{0:T(256)S(1)} %broadcast_multiply_fusion.1, f32[256,2]{1,0:T(8,128)S(1)} %get-tuple-element.17), kind=kLoop, calls=%fused_computation.8 | loop fusion | flops 5242880 | bytes 8391680 | tf_op jit(solution)/shard_map/convert_element_type | solution.py:58
  (6 shorter events, 0.1 us)
Async XLA Ops:
  0.6 31.1 %copy-start = (bf16[2,2048,256]{2,1,0:T(8,128)(2,1)S(1)}, bf16[2,2048,256]{2,1,0:T(8,128)(2,1)}, u32[]{:S(2)}) copy-start(bf16[2,2048,256]{2,1,0:T(8,128)(2,1)} %param.6) | copy-start | bytes 6291460
  27.9 3.8 %copy-start.3 = (f32[256]{0:T(256)S(1)}, f32[256]{0:T(256)}, u32[]{:S(2)}) copy-start(f32[256]{0:T(256)} %param.7) | copy-start | bytes 3076
  31.7 1.6 %copy-start.2 = (bf16[32,8,2,2048]{3,1,2,0:T(8,128)(2,1)S(1)}, bf16[32,8,2,2048]{3,1,2,0:T(8,128)(2,1)}, u32[]{:S(2)}) copy-start(bf16[32,8,2,2048]{3,1,2,0:T(8,128)(2,1)} %copy.13) | copy-start | bytes 6291460
  33.8 2.7 %collective-permute-start = (f32[64,4096]{1,0:T(8,128)S(1)}, f32[64,4096]{1,0:T(8,128)S(1)}, u32[]{:S(2)}, u32[]{:S(2)}) collective-permute-start(f32[64,4096]{1,0:T(8,128)S(1)} %subtract_dynamic-update-slice_fusion), channel_id=1, source_target_pairs={{0,1},{1,0},{2,3},{3,2},{4,5},{5,4},{6,7},{7,6},{8,9},{9,8},{10,11... | collective-permute-start | bytes 3145736 | tf_op jit(solution)/shard_map/ppermute | solution.py:36
  36.7 25.5 %collective-permute-start.1 = (f32[64,4096]{1,0:T(8,128)S(1)}, f32[64,4096]{1,0:T(8,128)S(1)}, u32[]{:S(2)}, u32[]{:S(2)}) collective-permute-start(f32[64,4096]{1,0:T(8,128)S(1)} %add.60), channel_id=1, source_target_pairs={{0,2},{1,3},{2,0},{3,1},{4,6},{5,7},{6,4},{7,5},{8,10},{9,11},{10,... | collective-permute-start | bytes 3145736 | tf_op jit(solution)/shard_map/ppermute | solution.py:36
  62.3 24.8 %copy-start.1 = (bf16[256,2,2048]{2,1,0:T(2,128)(2,1)S(1)}, bf16[256,2,2048]{2,1,0:T(2,128)(2,1)}, u32[]{:S(2)}) copy-start(bf16[256,2,2048]{2,1,0:T(2,128)(2,1)} %param.8) | copy-start | bytes 6291460
  62.3 24.6 %collective-permute-start.2 = (f32[64,4096]{1,0:T(8,128)S(1)}, f32[64,4096]{1,0:T(8,128)S(1)}, u32[]{:S(2)}, u32[]{:S(2)}) collective-permute-start(f32[64,4096]{1,0:T(8,128)S(1)} %add.61), channel_id=1, source_target_pairs={{0,4},{1,5},{2,6},{3,7},{4,0},{5,1},{6,2},{7,3},{8,12},{9,13},{10,... | collective-permute-start | bytes 3145736 | tf_op jit(solution)/shard_map/ppermute | solution.py:36
  87.1 47.1 %collective-permute-start.3 = (f32[64,4096]{1,0:T(8,128)S(1)}, f32[64,4096]{1,0:T(8,128)S(1)}, u32[]{:S(2)}, u32[]{:S(2)}) collective-permute-start(f32[64,4096]{1,0:T(8,128)S(1)} %add.62), channel_id=1, source_target_pairs={{0,8},{1,9},{2,10},{3,11},{4,12},{5,13},{6,14},{7,15},{8,0},{9,1},... | collective-permute-start | bytes 3145736 | tf_op jit(solution)/shard_map/ppermute | solution.py:36
